TPU v7x, 1024 devices: a whole 8x8x8 slice. The times are simulated.
1024 devices in a mesh: pipe: 8 (over z), dp: 4 (over x_lo, core), expert: 32 (over y, x_hi).
Axes of the slice: x: 8 (x_hi: 4, x_lo: 2; x = x_hi * 2 + x_lo), y: 8, z: 8, core: 2. Of those that a mesh axis runs over, the one named last changes fastest.
Arguments:
- cotangent: bfloat16 [8, 8192, 7168], P('pipe', ('dp', 'expert')), may hold values from -6 to 6
- routes: int32 [8, 2, 8192, 8], P('pipe', None, ('dp', 'expert')), may hold values from 0 to 255, as said below
- gates: bfloat16 [8, 2, 8192, 8], P('pipe', None, ('dp', 'expert')), may hold values from 0.099609375 to 1
- gate_pre: bfloat16 [8, 2, 4, 32, 2, 4096], P('pipe', None, 'dp', None, None, 'expert'), may hold values from -6 to 6
- up_pre: bfloat16 [8, 2, 4, 32, 2, 4096], P('pipe', None, 'dp', None, None, 'expert'), may hold values from -6 to 6
- w_gate: bfloat16 [8, 7168, 4096], P('pipe', None, 'expert'), may hold values from -0.0625 to 0.0625
- w_up: bfloat16 [8, 7168, 4096], P('pipe', None, 'expert'), may hold values from -0.0625 to 0.0625
- w_down: bfloat16 [8, 4096, 7168], P('pipe', 'expert'), may hold values from -0.125 to 0.125
Outputs:
- down_grad: float32 [8, 4096, 7168], P('pipe', 'expert', 'dp')
Inputs may be any that keep to these rules, and one draw needn't show every extreme that they name: `routes`: each token names 8 different experts. At one section and step the tokens of one device name each of the experts 0 to 1 at least once and at most 2 times; at every section and step, in some replica every device names one of them exactly 2 times.
All inputs are finite; a program needn't handle non-finite values.
Results may differ from a plain program's by a relative error of at most 0.0095.
Values may be sent and summed in bfloat16 or wider, within the bound.
No kernel may reach another device: no remote copies, remote signals or barrier semaphores. Data moves between devices by JAX's collectives and lax.ppermute only.
A program may use at most 64 MiB of HBM per device.

v0:
```python
import jax
import jax.numpy as jnp
from jax import lax
from jax.sharding import PartitionSpec as P

EXP_FL = 2
STEPS = 2


def side_by_side(arrays, axis, split_dim, concat_dim, along):
    widths = [a.shape[along] for a in arrays]
    both = jnp.concatenate(arrays, axis=along)
    filled = lax.all_to_all(both, axis, split_axis=split_dim, concat_axis=concat_dim, tiled=True)
    return tuple(jnp.split(filled, [sum(widths[:k]) for k in range(1, len(widths))], axis=along))


def shifted(block, axis, distance):
    devices = range(lax.axis_size(axis))
    route = [(i - distance, i) for i in devices if i - distance in devices]
    return lax.ppermute(block, axis, route)


def split_up(value, dim, size):
    before, after = (value.shape[:dim], value.shape[dim + 1 :])
    return jnp.moveaxis(value.reshape(*before, size, -1, *after), dim, 0)


def sent_and_summed(value, axis, dim):
    pieces = split_up(value, dim, lax.axis_size(axis))
    arrived = lax.all_to_all(pieces, axis, split_axis=0, concat_axis=0, tiled=True)
    return arrived.astype(jnp.float32).sum(axis=0)


def slot_tables(ids, weights, capacity):
    match = (ids[:, :, None] == jnp.arange(EXP_FL, dtype=jnp.int32)).astype(jnp.float32)
    hit = jnp.sum(match, axis=1)
    gate_sum = jnp.sum(match * weights.astype(jnp.float32)[:, :, None], axis=1)
    rank = jnp.cumsum(hit, axis=0) - 1.0
    slots = jnp.arange(capacity, dtype=jnp.float32)
    select = hit[:, :, None] * (rank[:, :, None] == slots).astype(jnp.float32)
    select = jnp.transpose(select, (1, 2, 0)).reshape(EXP_FL * capacity, ids.shape[0])
    slot_gate = jnp.sum(
        select.reshape(EXP_FL, capacity, ids.shape[0]) * jnp.transpose(gate_sum)[:, None, :], axis=2
    )
    return (select, slot_gate)


def contract_last(left, right):
    return lax.dot_general(
        left, right, (((1,), (1,)), ((), ())), preferred_element_type=jnp.float32
    )


def contract_first(left, right):
    return lax.dot_general(
        left, right, (((0,), (0,)), ((), ())), preferred_element_type=jnp.float32
    )


def body(cotangent, routes, gates, gate_pre, up_pre, w_gate, w_up, w_down):
    n_shards = lax.axis_size("expert")
    split = n_shards // EXP_FL
    width = cotangent.shape[2]
    capacity = gate_pre.shape[4]
    hidden = gate_pre.shape[5]
    gate_mat = w_gate[0]
    up_mat = w_up[0]
    down_mat = w_down[0]
    owner = jnp.arange(n_shards) // split
    grad_in = cotangent[0]
    total = jnp.zeros((hidden, width), jnp.float32)
    for step in range(STEPS):
        select, slot_gate = slot_tables(routes[0, step], gates[0, step], capacity)
        rows = jnp.dot(
            select.astype(jnp.bfloat16), grad_in, preferred_element_type=jnp.float32
        ).astype(jnp.bfloat16)
        send_rows = rows.reshape(EXP_FL, capacity * width)[owner]
        send_gate = slot_gate.astype(jnp.bfloat16)[owner]
        got_rows, got_gate = side_by_side((send_rows, send_gate), "expert", 0, 0, 1)
        flat_rows = got_rows.reshape(n_shards * capacity, width)
        gate_col = got_gate.reshape(n_shards * capacity, 1).astype(jnp.float32)
        pre_u = gate_pre[0, step, 0].reshape(n_shards * capacity, hidden).astype(jnp.float32)
        pre_v = up_pre[0, step, 0].reshape(n_shards * capacity, hidden).astype(jnp.float32)
        grad_act = gate_col * contract_last(flat_rows, down_mat)
        sig = jax.nn.sigmoid(pre_u)
        act = pre_u * sig
        dsilu = sig * (1.0 + pre_u * (1.0 - sig))
        d_gate = (grad_act * pre_v * dsilu).astype(jnp.bfloat16)
        d_up = (grad_act * act).astype(jnp.bfloat16)
        scaled = (gate_col * act * pre_v).astype(jnp.bfloat16)
        total = total + contract_first(scaled, flat_rows)
        if step + 1 < STEPS:
            partial_value = contract_last(d_gate, gate_mat) + contract_last(d_up, up_mat)
            partial_value = partial_value.astype(jnp.bfloat16).reshape(n_shards, capacity * width)
            returned = lax.all_to_all(
                partial_value, "expert", split_axis=0, concat_axis=0, tiled=True
            )
            summed = jnp.sum(
                returned.astype(jnp.float32).reshape(EXP_FL, split, capacity * width), axis=1
            )
            summed = summed.reshape(EXP_FL * capacity, width)
            spread = contract_first(select, summed)
            grad_out = grad_in.astype(jnp.float32) + spread
            grad_in = shifted(grad_out.astype(jnp.bfloat16), "pipe", -1)
    reduced = sent_and_summed(total.astype(jnp.bfloat16), "dp", 1)
    return reduced[None]


def solution(mesh):
    in_specs = (
        P("pipe", ("dp", "expert"), None),
        P("pipe", None, ("dp", "expert"), None),
        P("pipe", None, ("dp", "expert"), None),
        P("pipe", None, "dp", None, None, "expert"),
        P("pipe", None, "dp", None, None, "expert"),
        P("pipe", None, "expert"),
        P("pipe", None, "expert"),
        P("pipe", "expert", None),
    )
    out_specs = P("pipe", "expert", "dp")
    return jax.shard_map(body, mesh=mesh, in_specs=in_specs, out_specs=out_specs, check_vma=False)
```

profile of v0, /device:TPU:400, one launch (start us, length us, event | category | flops | bytes accessed | tf_op | source)
XLA Modules:
  0.0 249.3 jit_solution(17265199240418869994)
XLA Ops:
  0.0 0.0 copy-start
  0.0 0.8 slice_bitcast_fusion
  0.9 0.7 bitcast_convert_fusion
  1.6 0.1 copy.49
  1.7 0.1 reduce_window_sum.17
  1.8 0.1 copy.50
  1.9 0.1 multiply_reduce_fusion
  2.0 1.4 convolution_convert_fusion.1
  3.4 0.6 gather_fusion.1
  4.0 2.0 gather_fusion
  6.1 1.2 maximum_bitcast_fusion
  7.3 0.5 broadcast.235
  7.8 1.9 reduce
  9.8 0.0 copy-start.4
  9.8 3.5 %reshape.262 = bf16[32,2,7169]{2,1,0:T(2,128)(2,1)} reshape(bf16[32,14338]{1,0:T(8,128)(2,1)} %reduce) | data formatting | bytes 1835264
  13.3 13.0 %all-to-all-start = ((bf16[32,2,7169]{2,1,0:T(2,128)(2,1)}), bf16[32,2,7169]{2,1,0:T(2,128)(2,1)S(1)}, u32[]{:S(2)}, u32[]{:S(2)}) async-start(bf16[32,2,7169]{2,1,0:T(2,128)(2,1)} %reshape.262), calls=%async_computation | async-start | bytes 1867776 | tf_op jit(solution)/shard_map/all_to_all | solution.py:13
  26.2 0.0 copy-done.4
  26.3 0.0 copy-done.3
  26.3 31.6 %all-to-all-done = bf16[32,2,7169]{2,1,0:T(2,128)(2,1)S(1)} async-done(((bf16[32,2,7169]{2,1,0:T(2,128)(2,1)}), bf16[32,2,7169]{2,1,0:T(2,128)(2,1)S(1)}, u32[]{:S(2)}, u32[]{:S(2)}) %all-to-all-start) | async-done | bytes 917664 | tf_op jit(solution)/shard_map/all_to_all | solution.py:13
  57.9 2.4 reshape.263
  60.3 1.6 copy.66
  61.9 1.0 split.17
  62.9 1.5 reshape.219
  64.4 0.1 reshape.225
  64.5 2.2 fusion.8
  66.8 0.0 copy-done
  66.8 0.0 copy-start.2
  66.8 0.8 fusion.4
  67.6 0.7 copy-done.2
  68.3 1.7 fusion.2
  70.0 3.8 %all_to_all.34 = bf16[32,1,14336]{2,1,0:T(2,128)(2,1)} reshape(bf16[64,7168]{1,0:T(8,128)(2,1)} %fusion.2) | data formatting | bytes 1835008 | tf_op jit(solution)/shard_map/all_to_all | solution.py:95
  73.8 8.1 %reduce.1 = bf16[32,14336]{1,0:T(8,128)(2,1)} reduce(bf16[32,1,14336]{2,1,0:T(2,128)(2,1)} %all_to_all.34, bf16[]{:T(256)} %broadcast.235), dimensions={1}, to_apply=%all_to_all.34.reduce_sub_computation | reduce | bytes 1835010 | tf_op jit(solution)/shard_map/all_to_all | solution.py:95
  81.9 3.5 %reshape.264 = bf16[32,2,7168]{2,1,0:T(2,128)(2,1)} reshape(bf16[32,14336]{1,0:T(8,128)(2,1)} %reduce.1) | data formatting | bytes 1835008
  85.4 35.7 %all_to_all.39 = bf16[32,2,7168]{2,1,0:T(2,128)(2,1)} all-to-all(bf16[32,2,7168]{2,1,0:T(2,128)(2,1)} %reshape.264), channel_id=1, replica_groups=mesh['pipe'=8,'dp'=4,'expert'=32] {'expert'}, dimensions={0} | all-to-all | bytes 1835008 | tf_op jit(solution)/shard_map/all_to_all | solution.py:95
  121.1 6.1 %reshape.265 = bf16[32,1,14336]{2,1,0:T(2,128)(2,1)} reshape(bf16[32,2,7168]{2,1,0:T(2,128)(2,1)} %all_to_all.39) | data formatting | bytes 1835008
  127.2 3.3 %copy.58 = f32[32,1,14336]{2,0,1:T(8,128)} copy(bf16[32,1,14336]{2,1,0:T(2,128)(2,1)} %reshape.265) | data formatting | bytes 2752512
  130.5 1.8 reduce_sum.76
  132.4 2.6 %fusion.1 = bf16[64,7168]{1,0:T(8,128)(2,1)} fusion(bf16[4,64]{1,0:T(4,128)(2,1)S(1)} %bitcast.88, bf16[4,7168]{1,0:T(4,128)(2,1)S(1)} %reshape.220, bf16[1,64,7168]{2,1,0:T(8,128)(2,1)} %param.8), kind=kOutput, calls=%fused_computation.8 | convolution fusion | flops 5046272 | bytes 1892864 | tf_op jit(solution)/shard_map/dot_general | solution.py:55
  134.9 1.9 collective-permute-start
  136.9 0.1 eq.98
  136.9 0.1 copy.52
  137.0 0.1 reduce_window_sum.18
  137.1 0.1 copy.53
  137.2 0.1 fusion.20
  137.3 0.6 gather_fusion.3
  137.9 23.6 %collective-permute-done = bf16[64,7168]{1,0:T(8,128)(2,1)} collective-permute-done((bf16[64,7168]{1,0:T(8,128)(2,1)}, bf16[64,7168]{1,0:T(8,128)(2,1)}, u32[]{:S(2)}, u32[]{:S(2)}) %collective-permute-start) | collective-permute-done | bytes 917536 | tf_op jit(solution)/shard_map/ppermute | solution.py:20
  161.6 1.5 convolution_convert_fusion
  163.1 2.0 gather_fusion.2
  165.1 2.2 maximum_bitcast_fusion.1
  167.3 3.1 %reduce.2 = bf16[32,14338]{1,0:T(8,128)(2,1)} reduce(bf16[32,1,14338]{2,0,1:T(8,128)(2,1)} %maximum_bitcast_fusion.1, bf16[]{:T(256)} %broadcast.235), dimensions={1}, to_apply=%copy.55.reduce_sub_computation | reduce | bytes 1835266 | tf_op jit(solution)/shard_map/all_to_all | solution.py:13
  170.4 3.5 %reshape.266 = bf16[32,2,7169]{2,1,0:T(2,128)(2,1)} reshape(bf16[32,14338]{1,0:T(8,128)(2,1)} %reduce.2) | data formatting | bytes 1835264
  173.9 35.4 %all_to_all.40 = bf16[32,2,7169]{2,1,0:T(2,128)(2,1)} all-to-all(bf16[32,2,7169]{2,1,0:T(2,128)(2,1)} %reshape.266), channel_id=1, replica_groups=mesh['pipe'=8,'dp'=4,'expert'=32] {'expert'}, dimensions={0} | all-to-all | bytes 1835264 | tf_op jit(solution)/shard_map/all_to_all | solution.py:13
  209.3 6.4 %reshape.267 = bf16[32,1,14338]{2,1,0:T(2,128)(2,1)} reshape(bf16[32,2,7169]{2,1,0:T(2,128)(2,1)} %all_to_all.40) | data formatting | bytes 1835264
  215.8 1.6 copy.65
  217.4 1.0 split.19
  218.4 2.3 reshape.222
  220.7 0.1 fusion.16
  220.8 0.0 copy-start.1
  220.8 0.7 fusion.28
  221.5 0.5 copy-done.1
  222.0 0.7 fusion
  222.7 0.1 copy.64
  222.8 25.3 %all_to_all.41 = bf16[4,128,1792]{2,1,0:T(8,128)(2,1)S(1)} all-to-all(bf16[4,128,1792]{2,1,0:T(8,128)(2,1)S(1)} %bitcast.71), channel_id=1, replica_groups=mesh['pipe'=8,'dp'=4,'expert'=32] {'dp'}, dimensions={0} | all-to-all | bytes 3670016 | tf_op jit(solution)/shard_map/all_to_all | solution.py:30
  248.1 1.2 convert_reduce_fusion
  (17 shorter events, 0.2 us)
Async XLA Ops:
  0.0 66.8 %copy-start = (bf16[1,7168,128]{2,1,0:T(8,128)(2,1)S(1)}, bf16[1,7168,128]{2,1,0:T(8,128)(2,1)}, u32[]{:S(2)}) copy-start(bf16[1,7168,128]{2,1,0:T(8,128)(2,1)} %param.13) | copy-start | bytes 5505028
  9.8 16.5 %copy-start.4 = (bf16[1,2,1,32,2,128]{5,4,3,2,1,0:T(2,128)(2,1)S(1)}, bf16[1,2,1,32,2,128]{5,4,3,2,1,0:T(2,128)(2,1)}, u32[]{:S(2)}) copy-start(bf16[1,2,1,32,2,128]{5,4,3,2,1,0:T(2,128)(2,1)} %param.11) | copy-start | bytes 98308
  9.8 16.5 %copy-start.3 = (bf16[1,2,1,32,2,128]{5,4,3,2,1,0:T(2,128)(2,1)S(1)}, bf16[1,2,1,32,2,128]{5,4,3,2,1,0:T(2,128)(2,1)}, u32[]{:S(2)}) copy-start(bf16[1,2,1,32,2,128]{5,4,3,2,1,0:T(2,128)(2,1)} %param.12) | copy-start | bytes 98308
  13.3 44.6 %all-to-all-start = ((bf16[32,2,7169]{2,1,0:T(2,128)(2,1)}), bf16[32,2,7169]{2,1,0:T(2,128)(2,1)S(1)}, u32[]{:S(2)}, u32[]{:S(2)}) async-start(bf16[32,2,7169]{2,1,0:T(2,128)(2,1)} %reshape.262), calls=%async_computation | async-start | bytes 1867776 | tf_op jit(solution)/shard_map/all_to_all | solution.py:13
  66.8 1.5 copy-start.2
  134.9 26.6 %collective-permute-start = (bf16[64,7168]{1,0:T(8,128)(2,1)}, bf16[64,7168]{1,0:T(8,128)(2,1)}, u32[]{:S(2)}, u32[]{:S(2)}) collective-permute-start(bf16[64,7168]{1,0:T(8,128)(2,1)} %fusion.1), channel_id=1, source_target_pairs={{128,0},{256,128},{384,256},{512,384},{640,512},{768,640},{896,768... | collective-permute-start | bytes 2752520 | tf_op jit(solution)/shard_map/ppermute | solution.py:20
  220.8 1.2 copy-start.1
where the time goes:
time: 251 us; the launch traced here: 249 us
  blocking collectives  96.5 us (38%)
  waiting for transfers between devices  55.2 us (22%)
  local copies, waits for them, and re-layouts  50.3 us (20%)
  other arithmetic  20.9 us (8%)
  starting transfers between devices  14.9 us (6%)
  matrix products  11.5 us (5%)
    all_to_all x1, blocking collectives, body(): lax.all_to_all(partial_value, 'expert', split_axis=0, concat_axis=0, tile...  35.7 us
    all_to_all x1, blocking collectives, side_by_side(): lax.all_to_all(both, axis, split_axis=split_dim, concat_axis=concat_dim,...  35.4 us
    unnamed x19, local copies, waits for them, and re-layouts  33.2 us
    all_to_all x1, waiting for transfers between devices, side_by_side(): lax.all_to_all(both, axis, split_axis=split_dim, concat_axis=concat_dim,...  31.6 us
    all_to_all x1, blocking collectives, sent_and_summed(): lax.all_to_all(pieces, axis, split_axis=0, concat_axis=0, tiled=True)  25.3 us
    ppermute x1, waiting for transfers between devices, shifted(): return lax.ppermute(block, axis, route)  23.6 us
    all_to_all x1, starting transfers between devices, side_by_side(): lax.all_to_all(both, axis, split_axis=split_dim, concat_axis=concat_dim,...  13 us
    all_to_all x4, other arithmetic, side_by_side(): lax.all_to_all(both, axis, split_axis=split_dim, concat_axis=concat_dim,...  8.46 us
  transfers between devices with their start and end apart: 2, of which 2 were waited for; matrix products, arithmetic and copies ran while one was open for 0% of the time, Pallas kernels for 0%

commit v1 on v0

v1 whole, which is shorter than its diff:
```python
import jax
import jax.numpy as jnp
from jax import lax
from jax.experimental import pallas as pl
from jax.experimental.pallas import tpu as pltpu
from jax.sharding import PartitionSpec as P

EXP_FL = 2
N_DP = 4
F32 = jnp.float32
BF16 = jnp.bfloat16
VMEM = pl.BlockSpec(memory_space=pltpu.VMEM)
SMEM = pl.BlockSpec(memory_space=pltpu.SMEM)


def mm(a, b, ca, cb, precision=None):
    return lax.dot_general(
        a, b, (((ca,), (cb,)), ((), ())), preferred_element_type=F32, precision=precision
    )


def iota(shape, dim):
    return lax.broadcasted_iota(jnp.int32, shape, dim)


def slice_of(row):
    return (row >> 1) & 3


def select_kernel(ids_ref, gates_ref, cot_ref, pay_ref, sel_ref, up_ref):
    n, _, width = pay_ref.shape
    tokens = cot_ref.shape[0]
    row = iota((16, tokens), 0)
    slot = (row & 1).astype(F32)
    before = (iota((tokens, tokens), 0) <= iota((tokens, tokens), 1)).astype(BF16)

    def tables(step):
        ids = ids_ref[step]
        weights = gates_ref[step].astype(F32)
        hits, sums = [], []
        for e in range(EXP_FL):
            match = (ids == e).astype(F32)
            hits.append(jnp.sum(match, axis=0, keepdims=True))
            sums.append(jnp.sum(match * weights, axis=0, keepdims=True))
        hit = jnp.where(row < 8, hits[0], hits[1])
        gate = jnp.where(row < 8, sums[0], sums[1])
        rank = mm(hit.astype(BF16), before, 1, 0) - 1.0
        return hit * (rank == slot).astype(F32), gate

    sel0, gate0 = tables(0)
    sel1, gate1 = tables(1)
    sel_ref[...] = sel0.astype(BF16)
    up_ref[...] = (sel1 * gate1).astype(BF16)
    pick = sel0 * gate0
    rows = jnp.zeros((16, width), F32)
    for q in range(N_DP):
        left = jnp.where(slice_of(row) == q, pick, 0.0).astype(BF16)
        rows = rows + mm(left, cot_ref[:, q * width : (q + 1) * width], 1, 0)
    rows = rows.astype(BF16)
    for t in range(n):
        pay_ref[t] = rows[:8] if t < n // 2 else rows[8:]


def expert_kernel(
    me_ref, x_ref, u_ref, v_ref, wd_ref, wg_ref, wu_ref, ret_ref, x0_ref, x1_ref, x2_ref, x3_ref
):
    me = me_ref[0]
    rows, width = x_ref.shape
    slots = rows // N_DP
    hidden = wd_ref.shape[0]
    grad = jnp.zeros((rows, hidden), F32)
    part = slice_of(iota((rows, hidden), 0))
    for q in range(N_DP):
        term = mm(x_ref[...], wd_ref[:, q * width : (q + 1) * width], 1, 1)
        grad = jnp.where(part == q, term, grad)
    grad = grad.reshape(rows // 8, 8, hidden)
    grad = grad + pltpu.roll(grad, 4, 1)
    grad = grad + pltpu.roll(grad, 2, 1)
    grad = grad.reshape(rows, hidden)
    wide = iota((rows, slots), 0)
    spread = (iota((rows, slots), 1) == 2 * (wide >> 3) + (wide & 1)).astype(BF16)
    u = mm(spread, u_ref[0], 1, 0)
    v = mm(spread, v_ref[0], 1, 0)
    sig = jax.nn.sigmoid(u)
    d_gate = grad * v * sig * (1.0 + u * (1.0 - sig))
    d_up = grad * (u * sig)
    both = jnp.concatenate([d_gate, d_up], axis=1)
    part = slice_of(iota((rows, 2 * hidden), 0))
    lefts = [jnp.where(part == q, both, 0.0).astype(BF16) for q in range(N_DP)]
    tile = min(256, width)
    for n in range(width // tile):
        acc = jnp.zeros((rows, tile), F32)
        for q in range(N_DP):
            at = q * width + n * tile
            right = jnp.concatenate([wg_ref[at : at + tile], wu_ref[at : at + tile]], axis=1)
            acc = acc + mm(lefts[q], right, 1, 1)
        ret_ref[:, n * tile : (n + 1) * tile] = acc.astype(BF16)
    acts = []
    for step in range(2):
        u = u_ref[step].astype(F32)
        v = v_ref[step].astype(F32)
        acts.append((u * jax.nn.sigmoid(u) * v).astype(BF16))
    low = iota((slots, rows), 0)
    wide = iota((slots, rows), 1)
    mine = (low >> 1 == wide >> 3) & (low & 1 == wide & 1)
    for k, out_ref in enumerate((x0_ref, x1_ref, x2_ref, x3_ref)):
        pick = (mine & (slice_of(wide) == (me ^ k))).astype(BF16)
        out_ref[:, :width] = mm(pick, x_ref[...], 1, 0).astype(BF16)
        out_ref[:, width : width + hidden] = acts[0]
        out_ref[:, width + hidden :] = acts[1]


def combine_kernel(back_ref, up_ref, sel_ref, cot_ref, out_ref):
    n, _, width = back_ref.shape
    sums = [jnp.sum(back_ref[e * (n // 2) : (e + 1) * (n // 2)].astype(F32), axis=0) for e in range(EXP_FL)]
    back = jnp.concatenate(sums, axis=0)
    up = up_ref[...]
    meet = mm(up, sel_ref[...], 1, 1)
    meet = jnp.where(slice_of(iota((16, 16), 0)) == slice_of(iota((16, 16), 1)), meet, 0.0)
    out = mm(meet, back, 1, 0, lax.Precision.HIGHEST)
    row = slice_of(iota(up.shape, 0))
    for q in range(N_DP):
        left = jnp.where(row == q, up, jnp.zeros_like(up))
        out = out + mm(left, cot_ref[:, q * width : (q + 1) * width], 1, 0)
    out_ref[...] = out.astype(BF16)


def first_kernel(x0_ref, x1_ref, x2_ref, x3_ref, out_ref):
    hidden, width = out_ref.shape
    acc = jnp.zeros((hidden, width), F32)
    for ref in (x0_ref, x1_ref, x2_ref, x3_ref):
        acc = acc + mm(ref[:, width : width + hidden], ref[:, :width], 0, 0)
    out_ref[...] = acc


def second_kernel(me_ref, acc_ref, y_ref, x0_ref, x1_ref, x2_ref, x3_ref, out_ref):
    me = me_ref[0]
    hidden, width = out_ref.shape
    slots = x0_ref.shape[0]
    acc = acc_ref[...]
    for k, ref in enumerate((x0_ref, x1_ref, x2_ref, x3_ref)):
        at = pl.multiple_of((me ^ k) * slots, slots)
        acc = acc + mm(ref[:, width + hidden :], y_ref[pl.ds(at, slots), :], 0, 0)
    out_ref[...] = acc


def call(kernel, outs, specs, flops, moved, name):
    return pl.pallas_call(
        kernel,
        out_shape=outs,
        in_specs=specs,
        out_specs=jax.tree.map(lambda _: VMEM, outs),
        cost_estimate=pl.CostEstimate(flops=flops, bytes_accessed=moved, transcendentals=0),
        name=name,
    )


def like(shape, dtype=BF16):
    return jax.ShapeDtypeStruct(shape, dtype)


def body(cotangent, routes, gates, gate_pre, up_pre, w_gate, w_up, w_down):
    n = lax.axis_size("expert")
    pipe = lax.axis_size("pipe")
    cot = cotangent[0]
    tokens, full = cot.shape
    width = full // N_DP
    hidden = gate_pre.shape[5]
    slots = 2 * n
    me = lax.axis_index("dp").astype(jnp.int32).reshape(1)
    ids = jnp.swapaxes(routes[0], 1, 2)
    weights = jnp.swapaxes(gates[0], 1, 2)
    pay, sel0, up = call(
        select_kernel,
        (like((n, 8, width)), like((16, tokens)), like((16, tokens))),
        [VMEM] * 3,
        10**8,
        2 * 10**6,
        "select",
    )(ids, weights, cot)
    up = lax.ppermute(up, "pipe", [(i, i + 1) for i in range(pipe - 1)])
    got = lax.all_to_all(pay, "expert", 0, 0, tiled=True)
    u = gate_pre[0].reshape(2, slots, hidden)
    v = up_pre[0].reshape(2, slots, hidden)
    piece = like((slots, width + 2 * hidden))
    ret, x0, x1, x2, x3 = call(
        expert_kernel,
        (like((8 * n, width)), piece, piece, piece, piece),
        [SMEM] + [VMEM] * 6,
        2 * 10**9,
        8 * 10**6,
        "expert",
    )(me, got.reshape(8 * n, width), u, v, w_down[0], w_gate[0], w_up[0])
    back = lax.all_to_all(ret.reshape(n, 8, width), "expert", 0, 0, tiled=True)
    rows = call(combine_kernel, like((16, width)), [VMEM] * 4, 10**8, 2 * 10**6, "combine")(
        back, up, sel0, cot
    )
    rows = lax.ppermute(rows, "pipe", [(i, i - 1) for i in range(1, pipe)])
    x1 = lax.ppermute(x1, "dp", [(i, i ^ 1) for i in range(N_DP)])
    x2 = lax.ppermute(x2, "dp", [(i, i ^ 2) for i in range(N_DP)])
    x3 = lax.ppermute(x3, "dp", [(i, i ^ 3) for i in range(N_DP)])
    rows = rows.reshape(EXP_FL, N_DP, 1, 2, width).swapaxes(0, 1)
    rows = jnp.broadcast_to(rows, (N_DP, EXP_FL, n // EXP_FL, 2, width))
    got = lax.all_to_all(rows.reshape(N_DP * n, 2, width), ("dp", "expert"), 0, 0, tiled=True)
    acc = call(first_kernel, like((hidden, width), F32), [VMEM] * 4, 10**8, 2 * 10**6, "first")(
        x0, x1, x2, x3
    )
    out = call(
        second_kernel, like((hidden, width), F32), [SMEM] + [VMEM] * 6, 10**8, 2 * 10**6, "second"
    )(me, acc, got.reshape(N_DP * slots, width), x0, x1, x2, x3)
    return out[None]


def solution(mesh):
    in_specs = (
        P("pipe", ("dp", "expert"), None),
        P("pipe", None, ("dp", "expert"), None),
        P("pipe", None, ("dp", "expert"), None),
        P("pipe", None, "dp", None, None, "expert"),
        P("pipe", None, "dp", None, None, "expert"),
        P("pipe", None, "expert"),
        P("pipe", None, "expert"),
        P("pipe", "expert", None),
    )
    out_specs = P("pipe", "expert", "dp")
    return jax.shard_map(body, mesh=mesh, in_specs=in_specs, out_specs=out_specs, check_vma=False)
```

time: 251 us -> 154 us (0.61)
  the two profiles are of different devices: /device:TPU:400 before, /device:TPU:385 now
where the time goes in v1:
time: 154 us; the launch traced here: 153 us
  waiting for transfers between devices  79.2 us (51%)
  starting transfers between devices  50.8 us (33%)
  Pallas kernels  17.9 us (12%)
  local copies, waits for them, and re-layouts  5.37 us (3%)
    all_to_all x1, waiting for transfers between devices, body(): got = lax.all_to_all(pay, 'expert', 0, 0, tiled=True)  28.1 us
    all_to_all x1, waiting for transfers between devices, body(): back = lax.all_to_all(ret.reshape(n, 8, width), 'expert', 0, 0, tiled=True)  19.7 us
    ppermute x1, waiting for transfers between devices, body(): x2 = lax.ppermute(x2, 'dp', [(i, i ^ 2) for i in range(N_DP)])  19.1 us
    all_to_all x1, starting transfers between devices, body(): got = lax.all_to_all(pay, 'expert', 0, 0, tiled=True)  12.6 us
    all_to_all x1, starting transfers between devices, body(): lax.all_to_all(rows.reshape(N_DP * n, 2, width), ('dp', 'expert'), 0, 0,...  12.4 us
    all_to_all x1, starting transfers between devices, body(): back = lax.all_to_all(ret.reshape(n, 8, width), 'expert', 0, 0, tiled=True)  9.53 us
    pallas_call x1, Pallas kernels, body(): call(expert_kernel, (like((8 * n, width)), piece, piece, piece, piece), [...  6.7 us
    ppermute x1, starting transfers between devices, body(): up = lax.ppermute(up, 'pipe', [(i, i + 1) for i in range(pipe - 1)])  6.11 us
  transfers between devices with their start and end apart: 8, of which 6 were waited for; matrix products, arithmetic and copies ran while one was open for 0% of the time, Pallas kernels for 2%

profile of v1, /device:TPU:385, one launch (start us, length us, event | category | flops | bytes accessed | tf_op | source)
XLA Modules:
  0.0 153.5 jit_solution(15442513091284921353)
XLA Ops:
  0.0 2.5 %select.1 = (bf16[32,8,1792]{2,1,0:T(8,128)(2,1)}, bf16[16,64]{1,0:T(8,128)(2,1)}, bf16[16,64]{1,0:T(8,128)(2,1)}) custom-call(s32[2,8,64]{2,1,0:T(8,128)} %bitcast.25, bf16[2,8,64]{2,1,0:T(8,128)(2,1)} %bitcast.26, bf16[64,7168]{1,0:T(8,128)(2,1)} %bitcast.20), custom_call_target="tpu_custom_call" | custom-call | flops 100000000 | bytes 2000000 | tf_op jit(solution)/shard_map/select/pallas_call | solution.py:173
  2.5 12.6 %all-to-all-start = ((bf16[32,8,1792]{2,1,0:T(8,128)(2,1)}), bf16[32,8,1792]{2,1,0:T(8,128)(2,1)S(1)}, u32[]{:S(2)}, u32[]{:S(2)}) async-start(bf16[32,8,1792]{2,1,0:T(8,128)(2,1)} %get-tuple-element.13), calls=%async_computation | async-start | bytes 1835008 | tf_op jit(solution)/shard_map/all_to_all | solution.py:182
  15.1 28.1 %all-to-all-done = bf16[32,8,1792]{2,1,0:T(8,128)(2,1)S(1)} async-done(((bf16[32,8,1792]{2,1,0:T(8,128)(2,1)}), bf16[32,8,1792]{2,1,0:T(8,128)(2,1)S(1)}, u32[]{:S(2)}, u32[]{:S(2)}) %all-to-all-start) | async-done | bytes 917536 | tf_op jit(solution)/shard_map/all_to_all | solution.py:182
  43.3 0.0 copy-start.4
  43.3 0.9 copy-done.4
  44.2 6.7 %expert.1 = (bf16[256,1792]{1,0:T(8,128)(2,1)}, bf16[64,2048]{1,0:T(8,128)(2,1)}, bf16[64,2048]{1,0:T(8,128)(2,1)}, bf16[64,2048]{1,0:T(8,128)(2,1)}, bf16[64,2048]{1,0:T(8,128)(2,1)}) custom-call(s32[1]{0:T(128)} %bitcast.me_ref, bf16[256,1792]{1,0:T(8,128)(2,1)} %bitcast.22, bf16[2,64,128]{2,1,0:T(8,128)(2,1)} %bitcast.30, bf16[2,64,128]{2,1,0:T(8,128)(2,1)} %bitcast.31, ...), custom_call_target="tpu_custom_call" | custom-call | flops 2000000000 | bytes 8000000 | tf_op jit(solution)/shard_map/expert/pallas_call | solution.py:186
  50.9 0.0 copy-start.9
  50.9 9.5 %all-to-all-start.1 = ((bf16[32,8,1792]{2,1,0:T(8,128)(2,1)}), bf16[32,8,1792]{2,1,0:T(8,128)(2,1)S(1)}, u32[]{:S(2)}, u32[]{:S(2)}) async-start(bf16[32,8,1792]{2,1,0:T(8,128)(2,1)} %bitcast.23), calls=%async_computation.1 | async-start | bytes 1835008 | tf_op jit(solution)/shard_map/all_to_all | solution.py:194
  60.4 0.0 copy-done.9
  60.4 6.1 %collective-permute-start.3 = (bf16[16,64]{1,0:T(8,128)(2,1)S(1)}, bf16[16,64]{1,0:T(8,128)(2,1)S(1)}, u32[]{:S(2)}, u32[]{:S(2)}) collective-permute-start(bf16[16,64]{1,0:T(8,128)(2,1)S(1)} %copy-done.9), channel_id=1, source_target_pairs={{0,128},{128,256},{256,384},{384,512},{512,640},{640,768},{768,896... | collective-permute-start | bytes 6152 | tf_op jit(solution)/shard_map/ppermute | solution.py:181
  66.6 0.7 collective-permute-done.3.up_ref
  67.3 0.0 copy-start.5
  67.3 19.7 %all-to-all-done.1.back_ref = bf16[32,8,1792]{2,1,0:T(8,128)(2,1)S(1)} async-done(((bf16[32,8,1792]{2,1,0:T(8,128)(2,1)}), bf16[32,8,1792]{2,1,0:T(8,128)(2,1)S(1)}, u32[]{:S(2)}, u32[]{:S(2)}) %all-to-all-start.1) | async-done | bytes 917536 | tf_op jit(solution)/shard_map/all_to_all | solution.py:194
  87.0 0.0 copy-start
  87.0 0.0 copy-done.5
  87.0 0.9 copy-done
  87.9 2.6 %combine.1 = bf16[16,1792]{1,0:T(8,128)(2,1)} custom-call(bf16[32,8,1792]{2,1,0:T(8,128)(2,1)} %copy-done, bf16[16,64]{1,0:T(8,128)(2,1)} %copy-done.5, bf16[16,64]{1,0:T(8,128)(2,1)} %get-tuple-element.20.sel_ref, bf16[64,7168]{1,0:T(8,128)(2,1)} %bitcast.21), custom_call_target="tpu_custom_call" | custom-call | flops 100000000 | bytes 2000000 | tf_op jit(solution)/shard_map/combine/pallas_call | solution.py:195
  90.5 0.0 copy-start.8
  90.5 0.0 copy-start.7
  90.5 0.0 copy-start.6
  90.5 2.0 %collective-permute-start.4 = (bf16[16,1792]{1,0:T(8,128)(2,1)}, bf16[16,1792]{1,0:T(8,128)(2,1)S(1)}, u32[]{:S(2)}, u32[]{:S(2)}) collective-permute-start(bf16[16,1792]{1,0:T(8,128)(2,1)} %combine.1), channel_id=1, source_target_pairs={{128,0},{256,128},{384,256},{512,384},{640,512},{768,640},{896,768... | collective-permute-start | bytes 172040 | tf_op jit(solution)/shard_map/ppermute | solution.py:198
  92.6 5.9 %collective-permute-done.4 = bf16[16,1792]{1,0:T(8,128)(2,1)S(1)} collective-permute-done((bf16[16,1792]{1,0:T(8,128)(2,1)}, bf16[16,1792]{1,0:T(8,128)(2,1)S(1)}, u32[]{:S(2)}, u32[]{:S(2)}) %collective-permute-start.4) | collective-permute-done | bytes 57376 | tf_op jit(solution)/shard_map/ppermute | solution.py:198
  98.5 1.4 broadcast_in_dim.11
  99.9 12.4 %all-to-all-start.2 = ((bf16[128,2,1792]{2,1,0:T(2,128)(2,1)}), bf16[128,2,1792]{2,1,0:T(2,128)(2,1)S(1)}, u32[]{:S(2)}, u32[]{:S(2)}) async-start(bf16[128,2,1792]{2,1,0:T(2,128)(2,1)} %bitcast.15), calls=%async_computation.2 | async-start | bytes 1835008 | tf_op jit(solution)/shard_map/all_to_all | solution.py:204
  112.3 0.0 copy-done.8
  112.3 2.7 %collective-permute-start = (bf16[64,2048]{1,0:T(8,128)(2,1)S(1)}, bf16[64,2048]{1,0:T(8,128)(2,1)S(1)}, u32[]{:S(2)}, u32[]{:S(2)}) collective-permute-start(bf16[64,2048]{1,0:T(8,128)(2,1)S(1)} %copy-done.8), channel_id=1, source_target_pairs={{0,32},{32,0},{64,96},{96,64},{1,33},{33,1},{65,97},{97,65},{2,34}... | collective-permute-start | bytes 786440 | tf_op jit(solution)/shard_map/ppermute | solution.py:199
  115.0 0.0 copy-done.7
  115.0 3.1 %collective-permute-start.1 = (bf16[64,2048]{1,0:T(8,128)(2,1)S(1)}, bf16[64,2048]{1,0:T(8,128)(2,1)S(1)}, u32[]{:S(2)}, u32[]{:S(2)}) collective-permute-start(bf16[64,2048]{1,0:T(8,128)(2,1)S(1)} %copy-done.7), channel_id=1, source_target_pairs={{0,64},{32,96},{64,0},{96,32},{1,65},{33,97},{65,1},{97,33},{2,66}... | collective-permute-start | bytes 786440 | tf_op jit(solution)/shard_map/ppermute | solution.py:200
  118.1 0.0 copy-done.6
  118.1 2.4 %collective-permute-start.2 = (bf16[64,2048]{1,0:T(8,128)(2,1)S(1)}, bf16[64,2048]{1,0:T(8,128)(2,1)S(1)}, u32[]{:S(2)}, u32[]{:S(2)}) collective-permute-start(bf16[64,2048]{1,0:T(8,128)(2,1)S(1)} %copy-done.6), channel_id=1, source_target_pairs={{0,96},{32,64},{64,32},{96,0},{1,97},{33,65},{65,33},{97,1},{2,98}... | collective-permute-start | bytes 786440 | tf_op jit(solution)/shard_map/ppermute | solution.py:201
  120.5 0.0 collective-permute-done.x1_ref
  120.5 0.0 copy-start.1
  120.5 19.1 %collective-permute-done.1.x2_ref = bf16[64,2048]{1,0:T(8,128)(2,1)S(1)} collective-permute-done((bf16[64,2048]{1,0:T(8,128)(2,1)S(1)}, bf16[64,2048]{1,0:T(8,128)(2,1)S(1)}, u32[]{:S(2)}, u32[]{:S(2)}) %collective-permute-start.1) | collective-permute-done | bytes 262176 | tf_op jit(solution)/shard_map/ppermute | solution.py:200
  139.6 0.0 copy-start.2
  139.6 5.7 %collective-permute-done.2.x3_ref = bf16[64,2048]{1,0:T(8,128)(2,1)S(1)} collective-permute-done((bf16[64,2048]{1,0:T(8,128)(2,1)S(1)}, bf16[64,2048]{1,0:T(8,128)(2,1)S(1)}, u32[]{:S(2)}, u32[]{:S(2)}) %collective-permute-start.2) | collective-permute-done | bytes 262176 | tf_op jit(solution)/shard_map/ppermute | solution.py:201
  145.3 0.0 copy-start.3
  145.3 0.0 copy-done.1
  145.3 0.0 copy-done.2
  145.3 0.7 copy-done.3
  146.0 2.8 %first.1.acc_ref = f32[128,1792]{1,0:T(8,128)} custom-call(bf16[64,2048]{1,0:T(8,128)(2,1)} %get-tuple-element.14.x0_ref, bf16[64,2048]{1,0:T(8,128)(2,1)} %copy-done.1, bf16[64,2048]{1,0:T(8,128)(2,1)} %copy-done.2, bf16[64,2048]{1,0:T(8,128)(2,1)} %copy-done.3), custom_call_target="tpu_custom_call" | custom-call | flops 100000000 | bytes 2000000 | tf_op jit(solution)/shard_map/first/pallas_call | solution.py:205
  148.8 0.0 all-to-all-done.2
  148.8 1.3 reshape.23.y_ref
  150.1 3.3 %second.1 = f32[128,1792]{1,0:T(8,128)} custom-call(s32[1]{0:T(128)} %bitcast.me_ref, f32[128,1792]{1,0:T(8,128)} %first.1.acc_ref, bf16[256,1792]{1,0:T(8,128)(2,1)} %reshape.23.y_ref, bf16[64,2048]{1,0:T(8,128)(2,1)} %get-tuple-element.14.x0_ref, bf16[64,2048]{1,0:T(8,128)(2,1)} %copy-done.1, bf16[64,2048]{1,0:T(8,128)(2,1)} %copy-done.2, ...), custom_call_target="tpu_custom_call" | custom-call | flops 100000000 | bytes 2000000 | tf_op jit(solution)/shard_map/second/pallas_call | solution.py:208
  (2 shorter events, 0.1 us)
Async XLA Ops:
  2.5 40.7 %all-to-all-start = ((bf16[32,8,1792]{2,1,0:T(8,128)(2,1)}), bf16[32,8,1792]{2,1,0:T(8,128)(2,1)S(1)}, u32[]{:S(2)}, u32[]{:S(2)}) async-start(bf16[32,8,1792]{2,1,0:T(8,128)(2,1)} %get-tuple-element.13), calls=%async_computation | async-start | bytes 1835008 | tf_op jit(solution)/shard_map/all_to_all | solution.py:182
  43.3 0.9 copy-start.4
  50.9 9.5 %copy-start.9 = (bf16[16,64]{1,0:T(8,128)(2,1)S(1)}, bf16[16,64]{1,0:T(8,128)(2,1)}, u32[]{:S(2)}) copy-start(bf16[16,64]{1,0:T(8,128)(2,1)} %get-tuple-element.19) | copy-start | bytes 6148
  50.9 36.1 %all-to-all-start.1 = ((bf16[32,8,1792]{2,1,0:T(8,128)(2,1)}), bf16[32,8,1792]{2,1,0:T(8,128)(2,1)S(1)}, u32[]{:S(2)}, u32[]{:S(2)}) async-start(bf16[32,8,1792]{2,1,0:T(8,128)(2,1)} %bitcast.23), calls=%async_computation.1 | async-start | bytes 1835008 | tf_op jit(solution)/shard_map/all_to_all | solution.py:194
  60.4 6.9 %collective-permute-start.3 = (bf16[16,64]{1,0:T(8,128)(2,1)S(1)}, bf16[16,64]{1,0:T(8,128)(2,1)S(1)}, u32[]{:S(2)}, u32[]{:S(2)}) collective-permute-start(bf16[16,64]{1,0:T(8,128)(2,1)S(1)} %copy-done.9), channel_id=1, source_target_pairs={{0,128},{128,256},{256,384},{384,512},{512,640},{640,768},{768,896... | collective-permute-start | bytes 6152 | tf_op jit(solution)/shard_map/ppermute | solution.py:181
  67.3 19.7 %copy-start.5 = (bf16[16,64]{1,0:T(8,128)(2,1)}, bf16[16,64]{1,0:T(8,128)(2,1)S(1)}, u32[]{:S(2)}) copy-start(bf16[16,64]{1,0:T(8,128)(2,1)S(1)} %collective-permute-done.3.up_ref) | copy-start | bytes 6148
  87.0 0.9 copy-start
  90.5 21.8 %copy-start.8 = (bf16[64,2048]{1,0:T(8,128)(2,1)S(1)}, bf16[64,2048]{1,0:T(8,128)(2,1)}, u32[]{:S(2)}) copy-start(bf16[64,2048]{1,0:T(8,128)(2,1)} %get-tuple-element.15) | copy-start | bytes 786436
  90.5 24.5 %copy-start.7 = (bf16[64,2048]{1,0:T(8,128)(2,1)S(1)}, bf16[64,2048]{1,0:T(8,128)(2,1)}, u32[]{:S(2)}) copy-start(bf16[64,2048]{1,0:T(8,128)(2,1)} %get-tuple-element.16) | copy-start | bytes 786436
  90.5 27.6 %copy-start.6 = (bf16[64,2048]{1,0:T(8,128)(2,1)S(1)}, bf16[64,2048]{1,0:T(8,128)(2,1)}, u32[]{:S(2)}) copy-start(bf16[64,2048]{1,0:T(8,128)(2,1)} %get-tuple-element.17) | copy-start | bytes 786436
  90.5 7.9 %collective-permute-start.4 = (bf16[16,1792]{1,0:T(8,128)(2,1)}, bf16[16,1792]{1,0:T(8,128)(2,1)S(1)}, u32[]{:S(2)}, u32[]{:S(2)}) collective-permute-start(bf16[16,1792]{1,0:T(8,128)(2,1)} %combine.1), channel_id=1, source_target_pairs={{128,0},{256,128},{384,256},{512,384},{640,512},{768,640},{896,768... | collective-permute-start | bytes 172040 | tf_op jit(solution)/shard_map/ppermute | solution.py:198
  99.9 48.9 %all-to-all-start.2 = ((bf16[128,2,1792]{2,1,0:T(2,128)(2,1)}), bf16[128,2,1792]{2,1,0:T(2,128)(2,1)S(1)}, u32[]{:S(2)}, u32[]{:S(2)}) async-start(bf16[128,2,1792]{2,1,0:T(2,128)(2,1)} %bitcast.15), calls=%async_computation.2 | async-start | bytes 1835008 | tf_op jit(solution)/shard_map/all_to_all | solution.py:204
  112.3 8.2 %collective-permute-start = (bf16[64,2048]{1,0:T(8,128)(2,1)S(1)}, bf16[64,2048]{1,0:T(8,128)(2,1)S(1)}, u32[]{:S(2)}, u32[]{:S(2)}) collective-permute-start(bf16[64,2048]{1,0:T(8,128)(2,1)S(1)} %copy-done.8), channel_id=1, source_target_pairs={{0,32},{32,0},{64,96},{96,64},{1,33},{33,1},{65,97},{97,65},{2,34}... | collective-permute-start | bytes 786440 | tf_op jit(solution)/shard_map/ppermute | solution.py:199
  115.0 24.6 %collective-permute-start.1 = (bf16[64,2048]{1,0:T(8,128)(2,1)S(1)}, bf16[64,2048]{1,0:T(8,128)(2,1)S(1)}, u32[]{:S(2)}, u32[]{:S(2)}) collective-permute-start(bf16[64,2048]{1,0:T(8,128)(2,1)S(1)} %copy-done.7), channel_id=1, source_target_pairs={{0,64},{32,96},{64,0},{96,32},{1,65},{33,97},{65,1},{97,33},{2,66}... | collective-permute-start | bytes 786440 | tf_op jit(solution)/shard_map/ppermute | solution.py:200
  118.1 27.1 %collective-permute-start.2 = (bf16[64,2048]{1,0:T(8,128)(2,1)S(1)}, bf16[64,2048]{1,0:T(8,128)(2,1)S(1)}, u32[]{:S(2)}, u32[]{:S(2)}) collective-permute-start(bf16[64,2048]{1,0:T(8,128)(2,1)S(1)} %copy-done.6), channel_id=1, source_target_pairs={{0,96},{32,64},{64,32},{96,0},{1,97},{33,65},{65,33},{97,1},{2,98}... | collective-permute-start | bytes 786440 | tf_op jit(solution)/shard_map/ppermute | solution.py:201
  120.5 24.8 %copy-start.1 = (bf16[64,2048]{1,0:T(8,128)(2,1)}, bf16[64,2048]{1,0:T(8,128)(2,1)S(1)}, u32[]{:S(2)}) copy-start(bf16[64,2048]{1,0:T(8,128)(2,1)S(1)} %collective-permute-done.x1_ref) | copy-start | bytes 786436
  139.6 5.7 %copy-start.2 = (bf16[64,2048]{1,0:T(8,128)(2,1)}, bf16[64,2048]{1,0:T(8,128)(2,1)S(1)}, u32[]{:S(2)}) copy-start(bf16[64,2048]{1,0:T(8,128)(2,1)S(1)} %collective-permute-done.1.x2_ref) | copy-start | bytes 786436
  145.3 0.7 copy-start.3

commit v2 on v1

v2 whole, which is shorter than its diff:
```python
import jax
import jax.numpy as jnp
from jax import lax
from jax.experimental import pallas as pl
from jax.experimental.pallas import tpu as pltpu
from jax.sharding import PartitionSpec as P

EXP_FL = 2
N_DP = 4
F32 = jnp.float32
BF16 = jnp.bfloat16
VMEM = pl.BlockSpec(memory_space=pltpu.VMEM)
SMEM = pl.BlockSpec(memory_space=pltpu.SMEM)


def mm(a, b, ca, cb, precision=None):
    return lax.dot_general(
        a, b, (((ca,), (cb,)), ((), ())), preferred_element_type=F32, precision=precision
    )


def iota(shape, dim):
    return lax.broadcasted_iota(jnp.int32, shape, dim)


def slice_of(row):
    return (row >> 1) & 3


def select_kernel(ids_ref, gates_ref, cot_hbm, pay_ref, sel_ref, up_ref, cot_ref, sem):
    n, _, width = pay_ref.shape
    tokens = cot_ref.shape[0]
    copy = pltpu.make_async_copy(cot_hbm, cot_ref, sem)
    copy.start()
    row = iota((16, tokens), 0)
    slot = (row & 1).astype(F32)
    before = (iota((tokens, tokens), 0) <= iota((tokens, tokens), 1)).astype(BF16)

    def tables(step):
        ids = ids_ref[step]
        weights = gates_ref[step].astype(F32)
        hits, sums = [], []
        for e in range(EXP_FL):
            match = (ids == e).astype(F32)
            hits.append(jnp.sum(match, axis=0, keepdims=True))
            sums.append(jnp.sum(match * weights, axis=0, keepdims=True))
        hit = jnp.where(row < 8, hits[0], hits[1])
        gate = jnp.where(row < 8, sums[0], sums[1])
        rank = mm(hit.astype(BF16), before, 1, 0) - 1.0
        return hit * (rank == slot).astype(F32), gate

    sel0, gate0 = tables(0)
    sel1, gate1 = tables(1)
    sel_ref[...] = sel0.astype(BF16)
    up_ref[...] = (sel1 * gate1).astype(BF16)
    lefts = split(sel0 * gate0)
    copy.wait()
    rows = gathered(lefts, cot_ref, width).astype(BF16)
    for t in range(n):
        pay_ref[t] = rows[:8] if t < n // 2 else rows[8:]


def split(pick):
    row = slice_of(iota(pick.shape, 0))
    return [jnp.where(row == q, pick, 0.0).astype(BF16) for q in range(N_DP)]


def gathered(lefts, cot_ref, width):
    rows = mm(lefts[0], cot_ref[:, :width], 1, 0)
    for q in range(1, N_DP):
        rows = rows + mm(lefts[q], cot_ref[:, q * width : (q + 1) * width], 1, 0)
    return rows


def expert_kernel(
    me_ref,
    x_ref,
    u_ref,
    v_ref,
    wd_hbm,
    wg_hbm,
    wu_hbm,
    ret_ref,
    x0_ref,
    x1_ref,
    x2_ref,
    x3_ref,
    wd_ref,
    wg_ref,
    wu_ref,
    sems,
):
    copies = [
        pltpu.make_async_copy(src, dst, sems.at[k])
        for k, (src, dst) in enumerate(((wd_hbm, wd_ref), (wg_hbm, wg_ref), (wu_hbm, wu_ref)))
    ]
    for copy in copies:
        copy.start()
    me = me_ref[0]
    rows, width = x_ref.shape
    slots = rows // N_DP
    hidden = wd_ref.shape[0]
    acts = []
    for step in range(2):
        u = u_ref[step].astype(F32)
        v = v_ref[step].astype(F32)
        acts.append((u * jax.nn.sigmoid(u) * v).astype(BF16))
    low = iota((rows, rows), 0)
    wide = iota((rows, rows), 1)
    to = low // slots
    low = low - to * slots
    pick = (low >> 1 == wide >> 3) & (low & 1 == wide & 1) & (slice_of(wide) == (me ^ to))
    moved = mm(pick.astype(BF16), x_ref[...], 1, 0).astype(BF16)
    for k, out_ref in enumerate((x0_ref, x1_ref, x2_ref, x3_ref)):
        out_ref[:, :width] = moved[k * slots : (k + 1) * slots]
        out_ref[:, width : width + hidden] = acts[0]
        out_ref[:, width + hidden :] = acts[1]
    wide = iota((rows, slots), 0)
    spread = (iota((rows, slots), 1) == 2 * (wide >> 3) + (wide & 1)).astype(BF16)
    u = mm(spread, u_ref[0], 1, 0)
    v = mm(spread, v_ref[0], 1, 0)
    sig = jax.nn.sigmoid(u)
    for_gate = v * sig * (1.0 + u * (1.0 - sig))
    for_up = u * sig
    copies[0].wait()
    right = jnp.concatenate([wd_ref[:, q * width : (q + 1) * width] for q in range(N_DP)], axis=0)
    terms = mm(x_ref[...], right, 1, 1)
    part = slice_of(iota((rows, hidden), 0))
    grad = terms[:, :hidden]
    for q in range(1, N_DP):
        grad = jnp.where(part == q, terms[:, q * hidden : (q + 1) * hidden], grad)
    grad = grad.reshape(rows // 8, 8, hidden)
    grad = grad + pltpu.roll(grad, 4, 1)
    grad = grad + pltpu.roll(grad, 2, 1)
    grad = grad.reshape(rows, hidden)
    lefts = split(jnp.concatenate([grad * for_gate, grad * for_up], axis=1))
    copies[1].wait()
    copies[2].wait()
    tile = min(256, width)
    for n in range(width // tile):
        acc = None
        for q in range(N_DP):
            at = q * width + n * tile
            right = jnp.concatenate([wg_ref[at : at + tile], wu_ref[at : at + tile]], axis=1)
            term = mm(lefts[q], right, 1, 1)
            acc = term if acc is None else acc + term
        ret_ref[:, n * tile : (n + 1) * tile] = acc.astype(BF16)


def token_kernel(up_ref, sel_ref, cot_hbm, rows_ref, meet_ref, cot_ref, sem):
    copy = pltpu.make_async_copy(cot_hbm, cot_ref, sem)
    copy.start()
    up = up_ref[...]
    meet = mm(up, sel_ref[...], 1, 1)
    same = slice_of(iota((16, 16), 0)) == slice_of(iota((16, 16), 1))
    meet_ref[...] = jnp.where(same, meet, 0.0)
    copy.wait()
    rows_ref[...] = gathered(split(up.astype(F32)), cot_ref, rows_ref.shape[1])


def combine_kernel(back_ref, rows_ref, meet_ref, out_ref):
    n = back_ref.shape[0]
    half = n // EXP_FL
    sums = [jnp.sum(back_ref[e * half : (e + 1) * half].astype(F32), axis=0) for e in range(EXP_FL)]
    back = jnp.concatenate(sums, axis=0)
    out = rows_ref[...] + mm(meet_ref[...], back, 1, 0, lax.Precision.HIGHEST)
    out_ref[...] = out.astype(BF16)


def first_kernel(x0_ref, x1_ref, x2_ref, x3_ref, out_ref):
    hidden, width = out_ref.shape
    acc = None
    for ref in (x0_ref, x1_ref, x2_ref, x3_ref):
        term = mm(ref[:, width : width + hidden], ref[:, :width], 0, 0)
        acc = term if acc is None else acc + term
    out_ref[...] = acc


def second_kernel(me_ref, acc_ref, y_ref, x0_ref, x1_ref, x2_ref, x3_ref, out_ref):
    me = me_ref[0]
    hidden, width = out_ref.shape
    slots = x0_ref.shape[0]
    acc = acc_ref[...]
    for k, ref in enumerate((x0_ref, x1_ref, x2_ref, x3_ref)):
        at = pl.multiple_of((me ^ k) * slots, slots)
        acc = acc + mm(ref[:, width + hidden :], y_ref[pl.ds(at, slots), :], 0, 0)
    out_ref[...] = acc


def call(kernel, outs, flops, moved, ins, out_in_hbm=False, held=(), **kwargs):
    specs = [SMEM if x.dtype == jnp.int32 and x.ndim == 1 else VMEM for x in ins]
    specs[len(ins) - len(held) :] = [pl.BlockSpec(memory_space=pl.ANY)] * len(held)
    shapes = [like(*o) if out_in_hbm or not ON_CHIP else pltpu.VMEM(*o) for o in outs]
    return pl.pallas_call(
        kernel,
        out_shape=shapes,
        in_specs=specs,
        out_specs=[VMEM] * len(outs),
        cost_estimate=pl.CostEstimate(flops=flops, bytes_accessed=moved, transcendentals=0),
        compiler_params=pltpu.CompilerParams(vmem_limit_bytes=24 << 20),
        **kwargs,
    )(*ins)


def in_hbm(x):
    return pltpu.with_memory_space_constraint(x, pltpu.HBM) if ON_CHIP else x


def like(shape, dtype=BF16):
    return jax.ShapeDtypeStruct(shape, dtype)


ON_CHIP = True


def body(cotangent, routes, gates, gate_pre, up_pre, w_gate, w_up, w_down):
    n = lax.axis_size("expert")
    pipe = lax.axis_size("pipe")
    cot = cotangent[0]
    tokens, full = cot.shape
    width = full // N_DP
    hidden = gate_pre.shape[5]
    slots = 2 * n
    me = lax.axis_index("dp").astype(jnp.int32).reshape(1)
    ids = jnp.swapaxes(routes[0], 1, 2)
    weights = jnp.swapaxes(gates[0], 1, 2)
    pay, sel0, up = pl.pallas_call(
        select_kernel,
        out_shape=[(pltpu.VMEM if ON_CHIP else like)(s, BF16) for s in ((n, 8, width), (16, tokens), (16, tokens))],
        in_specs=[VMEM, VMEM, pl.BlockSpec(memory_space=pl.ANY)],
        out_specs=[VMEM] * 3,
        scratch_shapes=[pltpu.VMEM(cot.shape, BF16), pltpu.SemaphoreType.DMA(())],
        cost_estimate=pl.CostEstimate(flops=10**8, bytes_accessed=2 * 10**6, transcendentals=0),
        compiler_params=pltpu.CompilerParams(vmem_limit_bytes=24 << 20),
        name="select",
    )(ids, weights, in_hbm(cot))
    up = lax.ppermute(up, "pipe", [(i, i + 1) for i in range(pipe - 1)])
    got = lax.all_to_all(pay, "expert", 0, 0, tiled=True)
    u = gate_pre[0].reshape(2, slots, hidden)
    v = up_pre[0].reshape(2, slots, hidden)
    weights = [in_hbm(w[0]) for w in (w_down, w_gate, w_up)]
    piece = ((slots, width + 2 * hidden), BF16)
    ret, x0, x1, x2, x3 = call(
        expert_kernel,
        [((8 * n, width), BF16)] + [piece] * 4,
        2 * 10**9,
        8 * 10**6,
        (me, got.reshape(8 * n, width), u, v, *weights),
        held=weights,
        scratch_shapes=[pltpu.VMEM(w.shape, BF16) for w in weights] + [pltpu.SemaphoreType.DMA((3,))],
    )
    rows, meet = call(
        token_kernel, [((16, width), F32), ((16, 16), F32)], 10**9, 10**6, (up, sel0, in_hbm(cot)),
        held=[cot], scratch_shapes=[pltpu.VMEM(cot.shape, BF16), pltpu.SemaphoreType.DMA(())],
    )
    back = lax.all_to_all(ret.reshape(n, 8, width), "expert", 0, 0, tiled=True)
    (rows,) = call(combine_kernel, [((16, width), BF16)], 10**8, 10**6, (back, rows, meet))
    rows = lax.ppermute(rows, "pipe", [(i, i - 1) for i in range(1, pipe)])
    x1 = lax.ppermute(x1, "dp", [(i, i ^ 1) for i in range(N_DP)])
    x2 = lax.ppermute(x2, "dp", [(i, i ^ 2) for i in range(N_DP)])
    x3 = lax.ppermute(x3, "dp", [(i, i ^ 3) for i in range(N_DP)])
    rows = rows.reshape(EXP_FL, N_DP, 1, 2, width).swapaxes(0, 1)
    rows = jnp.broadcast_to(rows, (N_DP, EXP_FL, n // EXP_FL, 2, width))
    rows = rows.reshape(N_DP * n, 2, width)
    got = lax.all_to_all(rows, ("dp", "expert"), 0, 0, tiled=True)
    (acc,) = call(first_kernel, [((hidden, width), F32)], 10**8, 2 * 10**6, (x0, x1, x2, x3))
    (out,) = call(
        second_kernel,
        [((hidden, width), F32)],
        10**8,
        2 * 10**6,
        (me, acc, got.reshape(N_DP * slots, width), x0, x1, x2, x3),
        out_in_hbm=True,
    )
    return out[None]


def solution(mesh):
    in_specs = (
        P("pipe", ("dp", "expert"), None),
        P("pipe", None, ("dp", "expert"), None),
        P("pipe", None, ("dp", "expert"), None),
        P("pipe", None, "dp", None, None, "expert"),
        P("pipe", None, "dp", None, None, "expert"),
        P("pipe", None, "expert"),
        P("pipe", None, "expert"),
        P("pipe", "expert", None),
    )
    out_specs = P("pipe", "expert", "dp")

    return jax.shard_map(body, mesh=mesh, in_specs=in_specs, out_specs=out_specs, check_vma=False)
```

time: 154 us -> 146 us (0.948)
  Pallas kernels: 17.9 us -> 11.4 us
  waiting for transfers between devices: 79.2 us -> 77.2 us
    pallas_call x5 -> x6, Pallas kernels: 17.9 us -> 11.4 us  [the longest x5 9 us: call(): pl.pallas_call(kernel, out_shape=shapes, in_specs=specs, out_specs=[VMEM]...]
    all_to_all x1, waiting for transfers between devices: 19.7 us -> 18.2 us  [body(): back = lax.all_to_all(ret.reshape(n, 8, width), 'expert', 0, 0, tiled=True)]
  transfers between devices with their start and end apart: 8 -> 8, of which waited for: 6 -> 6; matrix products, arithmetic and copies ran while one was open for 0% -> 0% of each run, Pallas kernels for 2% -> 1%
where the time goes in v2:
time: 146 us; the launch traced here: 145 us
  waiting for transfers between devices  77.2 us (53%)
  starting transfers between devices  50.9 us (35%)
  Pallas kernels  11.4 us (8%)
  local copies, waits for them, and re-layouts  5.32 us (4%)
    all_to_all x1, waiting for transfers between devices, body(): got = lax.all_to_all(pay, 'expert', 0, 0, tiled=True)  28.1 us
    ppermute x1, waiting for transfers between devices, body(): x2 = lax.ppermute(x2, 'dp', [(i, i ^ 2) for i in range(N_DP)])  18.7 us
    all_to_all x1, waiting for transfers between devices, body(): back = lax.all_to_all(ret.reshape(n, 8, width), 'expert', 0, 0, tiled=True)  18.2 us
    all_to_all x1, starting transfers between devices, body(): got = lax.all_to_all(rows, ('dp', 'expert'), 0, 0, tiled=True)  12.7 us
    all_to_all x1, starting transfers between devices, body(): got = lax.all_to_all(pay, 'expert', 0, 0, tiled=True)  12.6 us
    all_to_all x1, starting transfers between devices, body(): back = lax.all_to_all(ret.reshape(n, 8, width), 'expert', 0, 0, tiled=True)  9.4 us
    pallas_call x5, Pallas kernels, call(): pl.pallas_call(kernel, out_shape=shapes, in_specs=specs, out_specs=[VMEM]...  9 us
    ppermute x1, starting transfers between devices, body(): up = lax.ppermute(up, 'pipe', [(i, i + 1) for i in range(pipe - 1)])  6.12 us
  transfers between devices with their start and end apart: 8, of which 6 were waited for; matrix products, arithmetic and copies ran while one was open for 0% of the time, Pallas kernels for 1%

profile of v2, /device:TPU:385, one launch (start us, length us, event | category | flops | bytes accessed | tf_op | source)
XLA Modules:
  0.0 145.0 jit_solution(14351894068094740650)
XLA Ops:
  0.0 0.0 copy-start
  0.0 0.7 copy-done
  0.7 0.0 copy-start.1
  0.7 0.7 copy-done.1
  1.4 0.0 copy-start.2
  1.4 0.0 copy-start.3
  1.4 2.4 %select.1 = (bf16[32,8,1792]{2,1,0:T(8,128)(2,1)}, bf16[16,64]{1,0:T(8,128)(2,1)S(1)}, bf16[16,64]{1,0:T(8,128)(2,1)S(1)}) custom-call(s32[2,8,64]{2,1,0:T(8,128)S(1)} %bitcast.21, bf16[2,8,64]{2,1,0:T(8,128)(2,1)S(1)} %bitcast.22, bf16[64,7168]{1,0:T(8,128)(2,1)} %bitcast.25), custom_call_target="tpu_custom_call" | custom-call | flops 100000000 | bytes 2000000 | tf_op jit(solution)/shard_map/select/pallas_call | solution.py:227
  3.8 12.6 %all-to-all-start = ((bf16[32,8,1792]{2,1,0:T(8,128)(2,1)}), bf16[32,8,1792]{2,1,0:T(8,128)(2,1)S(1)}, u32[]{:S(2)}, u32[]{:S(2)}) async-start(bf16[32,8,1792]{2,1,0:T(8,128)(2,1)} %get-tuple-element.15), calls=%async_computation | async-start | bytes 1835008 | tf_op jit(solution)/shard_map/all_to_all | solution.py:238
  16.4 28.1 %all-to-all-done = bf16[32,8,1792]{2,1,0:T(8,128)(2,1)S(1)} async-done(((bf16[32,8,1792]{2,1,0:T(8,128)(2,1)}), bf16[32,8,1792]{2,1,0:T(8,128)(2,1)S(1)}, u32[]{:S(2)}, u32[]{:S(2)}) %all-to-all-start) | async-done | bytes 917536 | tf_op jit(solution)/shard_map/all_to_all | solution.py:238
  44.5 0.0 copy-done.2
  44.5 0.0 copy-done.3
  44.5 5.0 %shard_map.82 = (bf16[256,1792]{1,0:T(8,128)(2,1)}, bf16[64,2048]{1,0:T(8,128)(2,1)S(1)}, bf16[64,2048]{1,0:T(8,128)(2,1)S(1)}, bf16[64,2048]{1,0:T(8,128)(2,1)S(1)}, bf16[64,2048]{1,0:T(8,128)(2,1)S(1)}) custom-call(s32[1]{0:T(128)} %bitcast.me_ref, bf16[256,1792]{1,0:T(8,128)(2,1)S(1)} %bitcast.20, bf16[2,64,128]{2,1,0:T(8,128)(2,1)S(1)} %bitcast.23, ...), custom_call_target="tpu_custom_call" | custom-call | flops 2000000000 | bytes 8000000 | tf_op jit(solution)/shard_map/pallas_call | solution.py:194
  49.5 9.4 %all-to-all-start.1 = ((bf16[32,8,1792]{2,1,0:T(8,128)(2,1)}), bf16[32,8,1792]{2,1,0:T(8,128)(2,1)S(1)}, u32[]{:S(2)}, u32[]{:S(2)}) async-start(bf16[32,8,1792]{2,1,0:T(8,128)(2,1)} %bitcast.12), calls=%async_computation.1 | async-start | bytes 1835008 | tf_op jit(solution)/shard_map/all_to_all | solution.py:256
  58.9 6.1 %collective-permute-start.3 = (bf16[16,64]{1,0:T(8,128)(2,1)S(1)}, bf16[16,64]{1,0:T(8,128)(2,1)S(1)}, u32[]{:S(2)}, u32[]{:S(2)}) collective-permute-start(bf16[16,64]{1,0:T(8,128)(2,1)S(1)} %get-tuple-element.21), channel_id=1, source_target_pairs={{0,128},{128,256},{256,384},{384,512},{512,640},{640,768},{768,896... | collective-permute-start | bytes 6152 | tf_op jit(solution)/shard_map/ppermute | solution.py:237
  65.1 0.7 collective-permute-done.3.up_ref
  65.8 1.4 shard_map.84
  67.2 18.2 %all-to-all-done.1.back_ref = bf16[32,8,1792]{2,1,0:T(8,128)(2,1)S(1)} async-done(((bf16[32,8,1792]{2,1,0:T(8,128)(2,1)}), bf16[32,8,1792]{2,1,0:T(8,128)(2,1)S(1)}, u32[]{:S(2)}, u32[]{:S(2)}) %all-to-all-start.1) | async-done | bytes 917536 | tf_op jit(solution)/shard_map/all_to_all | solution.py:256
  85.4 0.4 shard_map.85
  85.8 1.9 %collective-permute-start.4 = (bf16[16,1792]{1,0:T(8,128)(2,1)S(1)}, bf16[16,1792]{1,0:T(8,128)(2,1)S(1)}, u32[]{:S(2)}, u32[]{:S(2)}) collective-permute-start(bf16[16,1792]{1,0:T(8,128)(2,1)S(1)} %shard_map.85), channel_id=1, source_target_pairs={{128,0},{256,128},{384,256},{512,384},{640,512},{768,640},{896,768... | collective-permute-start | bytes 172040 | tf_op jit(solution)/shard_map/ppermute | solution.py:258
  87.7 5.9 %collective-permute-done.4 = bf16[16,1792]{1,0:T(8,128)(2,1)S(1)} collective-permute-done((bf16[16,1792]{1,0:T(8,128)(2,1)S(1)}, bf16[16,1792]{1,0:T(8,128)(2,1)S(1)}, u32[]{:S(2)}, u32[]{:S(2)}) %collective-permute-start.4) | collective-permute-done | bytes 57376 | tf_op jit(solution)/shard_map/ppermute | solution.py:258
  93.6 1.4 broadcast_in_dim.11
  95.0 12.7 %all-to-all-start.2 = ((bf16[128,2,1792]{2,1,0:T(2,128)(2,1)}), bf16[128,2,1792]{2,1,0:T(2,128)(2,1)}, u32[]{:S(2)}, u32[]{:S(2)}) async-start(bf16[128,2,1792]{2,1,0:T(2,128)(2,1)} %bitcast.15), calls=%async_computation.2 | async-start | bytes 1835008 | tf_op jit(solution)/shard_map/all_to_all | solution.py:265
  107.7 2.8 %collective-permute-start = (bf16[64,2048]{1,0:T(8,128)(2,1)S(1)}, bf16[64,2048]{1,0:T(8,128)(2,1)S(1)}, u32[]{:S(2)}, u32[]{:S(2)}) collective-permute-start(bf16[64,2048]{1,0:T(8,128)(2,1)S(1)} %get-tuple-element.17), channel_id=1, source_target_pairs={{0,32},{32,0},{64,96},{96,64},{1,33},{33,1},{65,97},{97,65},{2,34}... | collective-permute-start | bytes 786440 | tf_op jit(solution)/shard_map/ppermute | solution.py:259
  110.5 3.0 %collective-permute-start.1 = (bf16[64,2048]{1,0:T(8,128)(2,1)S(1)}, bf16[64,2048]{1,0:T(8,128)(2,1)S(1)}, u32[]{:S(2)}, u32[]{:S(2)}) collective-permute-start(bf16[64,2048]{1,0:T(8,128)(2,1)S(1)} %get-tuple-element.18), channel_id=1, source_target_pairs={{0,64},{32,96},{64,0},{96,32},{1,65},{33,97},{65,1},{97,33},{2,66}... | collective-permute-start | bytes 786440 | tf_op jit(solution)/shard_map/ppermute | solution.py:260
  113.5 2.4 %collective-permute-start.2 = (bf16[64,2048]{1,0:T(8,128)(2,1)S(1)}, bf16[64,2048]{1,0:T(8,128)(2,1)S(1)}, u32[]{:S(2)}, u32[]{:S(2)}) collective-permute-start(bf16[64,2048]{1,0:T(8,128)(2,1)S(1)} %get-tuple-element.19), channel_id=1, source_target_pairs={{0,96},{32,64},{64,32},{96,0},{1,97},{33,65},{65,33},{97,1},{2,98}... | collective-permute-start | bytes 786440 | tf_op jit(solution)/shard_map/ppermute | solution.py:261
  116.0 0.0 collective-permute-done.x1_ref
  116.0 18.7 %collective-permute-done.1.x2_ref = bf16[64,2048]{1,0:T(8,128)(2,1)S(1)} collective-permute-done((bf16[64,2048]{1,0:T(8,128)(2,1)S(1)}, bf16[64,2048]{1,0:T(8,128)(2,1)S(1)}, u32[]{:S(2)}, u32[]{:S(2)}) %collective-permute-start.1) | collective-permute-done | bytes 262176 | tf_op jit(solution)/shard_map/ppermute | solution.py:260
  134.7 5.6 %collective-permute-done.2.x3_ref = bf16[64,2048]{1,0:T(8,128)(2,1)S(1)} collective-permute-done((bf16[64,2048]{1,0:T(8,128)(2,1)S(1)}, bf16[64,2048]{1,0:T(8,128)(2,1)S(1)}, u32[]{:S(2)}, u32[]{:S(2)}) %collective-permute-start.2) | collective-permute-done | bytes 262176 | tf_op jit(solution)/shard_map/ppermute | solution.py:261
  140.3 0.7 shard_map.83.acc_ref
  140.9 0.0 all-to-all-done.2
  141.0 2.5 %reshape.23.y_ref = bf16[256,1792]{1,0:T(8,128)(2,1)S(1)} reshape(bf16[128,2,1792]{2,1,0:T(2,128)(2,1)} %all-to-all-done.2) | data formatting | bytes 1835008 | tf_op jit(solution)/shard_map/reshape | solution.py:272
  143.4 1.6 %shard_map.86 = f32[128,1792]{1,0:T(8,128)} custom-call(s32[1]{0:T(128)} %bitcast.me_ref, f32[128,1792]{1,0:T(8,128)S(1)} %shard_map.83.acc_ref, bf16[256,1792]{1,0:T(8,128)(2,1)S(1)} %reshape.23.y_ref, bf16[64,2048]{1,0:T(8,128)(2,1)S(1)} %get-tuple-element.16.x0_ref, bf16[64,2048]{1,0:T(8,128)(2,1)S(1)} %collective-permute-done.x1_ref, ...), custom_call_target="tpu_custom_call" | custom-call | flops 100000000 | bytes 2000000 | tf_op jit(solution)/shard_map/pallas_call | solution.py:194
  (2 shorter events, 0.1 us)
Async XLA Ops:
  0.0 0.7 copy-start
  0.7 0.7 copy-start.1
  1.4 43.2 %copy-start.2 = (bf16[1,2,1,32,2,128]{5,4,3,2,1,0:T(2,128)(2,1)S(1)}, bf16[1,2,1,32,2,128]{5,4,3,2,1,0:T(2,128)(2,1)}, u32[]{:S(2)}) copy-start(bf16[1,2,1,32,2,128]{5,4,3,2,1,0:T(2,128)(2,1)} %param.11) | copy-start | bytes 98308
  1.4 43.2 %copy-start.3 = (bf16[1,2,1,32,2,128]{5,4,3,2,1,0:T(2,128)(2,1)S(1)}, bf16[1,2,1,32,2,128]{5,4,3,2,1,0:T(2,128)(2,1)}, u32[]{:S(2)}) copy-start(bf16[1,2,1,32,2,128]{5,4,3,2,1,0:T(2,128)(2,1)} %param.12) | copy-start | bytes 98308
  3.8 40.7 %all-to-all-start = ((bf16[32,8,1792]{2,1,0:T(8,128)(2,1)}), bf16[32,8,1792]{2,1,0:T(8,128)(2,1)S(1)}, u32[]{:S(2)}, u32[]{:S(2)}) async-start(bf16[32,8,1792]{2,1,0:T(8,128)(2,1)} %get-tuple-element.15), calls=%async_computation | async-start | bytes 1835008 | tf_op jit(solution)/shard_map/all_to_all | solution.py:238
  49.5 35.9 %all-to-all-start.1 = ((bf16[32,8,1792]{2,1,0:T(8,128)(2,1)}), bf16[32,8,1792]{2,1,0:T(8,128)(2,1)S(1)}, u32[]{:S(2)}, u32[]{:S(2)}) async-start(bf16[32,8,1792]{2,1,0:T(8,128)(2,1)} %bitcast.12), calls=%async_computation.1 | async-start | bytes 1835008 | tf_op jit(solution)/shard_map/all_to_all | solution.py:256
  58.9 6.9 %collective-permute-start.3 = (bf16[16,64]{1,0:T(8,128)(2,1)S(1)}, bf16[16,64]{1,0:T(8,128)(2,1)S(1)}, u32[]{:S(2)}, u32[]{:S(2)}) collective-permute-start(bf16[16,64]{1,0:T(8,128)(2,1)S(1)} %get-tuple-element.21), channel_id=1, source_target_pairs={{0,128},{128,256},{256,384},{384,512},{512,640},{640,768},{768,896... | collective-permute-start | bytes 6152 | tf_op jit(solution)/shard_map/ppermute | solution.py:237
  85.8 7.8 %collective-permute-start.4 = (bf16[16,1792]{1,0:T(8,128)(2,1)S(1)}, bf16[16,1792]{1,0:T(8,128)(2,1)S(1)}, u32[]{:S(2)}, u32[]{:S(2)}) collective-permute-start(bf16[16,1792]{1,0:T(8,128)(2,1)S(1)} %shard_map.85), channel_id=1, source_target_pairs={{128,0},{256,128},{384,256},{512,384},{640,512},{768,640},{896,768... | collective-permute-start | bytes 172040 | tf_op jit(solution)/shard_map/ppermute | solution.py:258
  95.0 45.9 %all-to-all-start.2 = ((bf16[128,2,1792]{2,1,0:T(2,128)(2,1)}), bf16[128,2,1792]{2,1,0:T(2,128)(2,1)}, u32[]{:S(2)}, u32[]{:S(2)}) async-start(bf16[128,2,1792]{2,1,0:T(2,128)(2,1)} %bitcast.15), calls=%async_computation.2 | async-start | bytes 1835008 | tf_op jit(solution)/shard_map/all_to_all | solution.py:265
  107.7 8.3 %collective-permute-start = (bf16[64,2048]{1,0:T(8,128)(2,1)S(1)}, bf16[64,2048]{1,0:T(8,128)(2,1)S(1)}, u32[]{:S(2)}, u32[]{:S(2)}) collective-permute-start(bf16[64,2048]{1,0:T(8,128)(2,1)S(1)} %get-tuple-element.17), channel_id=1, source_target_pairs={{0,32},{32,0},{64,96},{96,64},{1,33},{33,1},{65,97},{97,65},{2,34}... | collective-permute-start | bytes 786440 | tf_op jit(solution)/shard_map/ppermute | solution.py:259
  110.5 24.2 %collective-permute-start.1 = (bf16[64,2048]{1,0:T(8,128)(2,1)S(1)}, bf16[64,2048]{1,0:T(8,128)(2,1)S(1)}, u32[]{:S(2)}, u32[]{:S(2)}) collective-permute-start(bf16[64,2048]{1,0:T(8,128)(2,1)S(1)} %get-tuple-element.18), channel_id=1, source_target_pairs={{0,64},{32,96},{64,0},{96,32},{1,65},{33,97},{65,1},{97,33},{2,66}... | collective-permute-start | bytes 786440 | tf_op jit(solution)/shard_map/ppermute | solution.py:260
  113.5 26.8 %collective-permute-start.2 = (bf16[64,2048]{1,0:T(8,128)(2,1)S(1)}, bf16[64,2048]{1,0:T(8,128)(2,1)S(1)}, u32[]{:S(2)}, u32[]{:S(2)}) collective-permute-start(bf16[64,2048]{1,0:T(8,128)(2,1)S(1)} %get-tuple-element.19), channel_id=1, source_target_pairs={{0,96},{32,64},{64,32},{96,0},{1,97},{33,65},{65,33},{97,1},{2,98}... | collective-permute-start | bytes 786440 | tf_op jit(solution)/shard_map/ppermute | solution.py:261
